TPU v7x, 256 devices: a whole 4x4x8 slice. The times are simulated.
256 devices in a mesh: task: 32 (over x, z_hi, core), mp: 8 (over y, z_lo).
Axes of the slice: x: 4, y: 4, z: 8 (z_hi: 4, z_lo: 2; z = z_hi * 2 + z_lo), core: 2. Of those that a mesh axis runs over, the one named last changes fastest.
Arguments:
- hidden_in: bfloat16 [32768, 1024], P(('task', 'mp')), parts along dimension 0, may hold values from -16 to 16
- ff_gain: float32 [1024], replicated, may hold values from 0.5 to 1.5
- w_gate: bfloat16 [1024, 3072], P(None, 'mp'), may hold values from -0.1875 to 0.1875
- w_up: bfloat16 [1024, 3072], P(None, 'mp'), may hold values from -0.1875 to 0.1875
- w_out: bfloat16 [3072, 1024], P('mp'), may hold values from -0.109375 to 0.109375
- ff_rescale: float32 [98304], P(('task', 'mp')), parts along dimension 0, may hold values from 0.5 to 2
- final_gain: float32 [1024], replicated, may hold values from 0.5 to 1.5
- w_head: bfloat16 [1024, 16384], P(None, 'mp'), may hold values from -8 to 8
- targets: int32 [32768], P('task'), parts along dimension 0, may hold values from 0 to 16383
- lengths: int32 [128, 4], P('task'), parts along dimension 0, may hold values from 1 to 64, as said below
- labels: int32 [128], P('task'), parts along dimension 0, may hold values from 0 to 3
Outputs:
- scale_grad: float32 [98304], P(('task', 'mp')), parts along dimension 0
- loss_value: float32 [32], P('task'), parts along dimension 0
There are 32 independent parts, one for each index of `task`. A program takes and returns all parts, laid end to end along the dimension named above; an argument that names none is the same for every part. Nothing has to cross between parts.
Inputs may be any that keep to these rules, and one draw needn't show every extreme that they name: `lengths`: every answer choice has at least one target token.
All inputs are finite; a program needn't handle non-finite values.
Results may differ from a plain program's by a relative error of at most 0.0067.
Values may be sent and summed in bfloat16 or wider, within the bound.
A program may use at most 64 MiB of HBM per device.

v0:
```python
import jax
import jax.numpy as jnp
from jax import lax
from jax.sharding import PartitionSpec as P

epsilon = 1e-06


def sent_to_all(x, axis):
    copies = jnp.broadcast_to(x, (lax.axis_size(axis), *x.shape))
    return lax.all_to_all(copies, axis, split_axis=0, concat_axis=0, tiled=True)


def joined_along(pieces, dim):
    dims = list(pieces.shape[1:])
    dims[dim] *= pieces.shape[0]
    return jnp.moveaxis(pieces, 0, dim).reshape(dims)


def gathered_copies(x, axis, dim):
    pieces = sent_to_all(x, axis)
    return joined_along(pieces, dim)


def cut_along(x, dim, count):
    dims = x.shape
    pieces = x.reshape(*dims[:dim], count, dims[dim] // count, *dims[dim + 1 :])
    return jnp.moveaxis(pieces, dim, 0)


def summed_on_arrival(x, axis, dim):
    count = lax.axis_size(axis)
    pieces = lax.all_to_all(cut_along(x, dim, count), axis, 0, 0, tiled=True)
    return jnp.sum(pieces, axis=0)


def gathered_once(x, axis):
    leaves = jax.tree.leaves(x)
    turns = sorted(range(len(leaves)), key=lambda k: -leaves[k].size)
    width = (1, *leaves[turns[0]].shape)[-1]
    lines = [
        jnp.pad(leaves[k].reshape(-1), (0, -leaves[k].size % width)).reshape(-1, width)
        for k in turns
    ]
    both, at, found = (lax.all_gather(jnp.concatenate(lines), axis), 0, {})
    for k, line in zip(turns, lines):
        slab = both[:, at : at + len(line)].reshape(len(both), -1)
        found[k] = slab[:, : leaves[k].size].reshape(-1, *leaves[k].shape)
        at += len(line)
    numbers = iter(range(len(leaves)))
    return jax.tree.map(lambda _: found[next(numbers)], x)


def combined_all(x, axis, combine):
    everything = gathered_once(x, axis)
    initial = jax.tree.map(lambda part: part[0], everything)

    def lap(k, so_far):
        return combine(so_far, jax.tree.map(lambda part: part[k], everything))

    return lax.fori_loop(1, lax.axis_size(axis), lap, initial)


def rms_scale(values, gain):
    inverse = lax.rsqrt(jnp.mean(values * values, axis=-1, keepdims=True) + epsilon)
    return (values * inverse * gain, inverse)


def norm_back(values, inverse, gain, upstream):
    scaled = upstream * gain
    return inverse * scaled - values * inverse**3 * jnp.mean(
        scaled * values, axis=-1, keepdims=True
    )


def task_loss(log_probs, lengths, labels):
    examples, choices = lengths.shape
    length = log_probs.shape[0] // (examples * choices)
    number_type = log_probs.dtype
    shaped = log_probs.reshape(examples, choices, length)
    position = jnp.arange(length, dtype=jnp.int32)
    valid = (position[None, None, :] < lengths[:, :, None]).astype(number_type)
    counts = lengths.astype(number_type)
    summed = jnp.sum(shaped * valid, axis=-1)
    average = summed / counts
    correct = (jnp.arange(choices, dtype=jnp.int32)[None, :] == labels[:, None]).astype(number_type)
    wrong = 1.0 - correct
    likely = -jnp.sum(summed * correct) / jnp.sum(counts * correct)
    safe = jnp.where(valid > 0, shaped, -1.0)
    unlikely = -jnp.sum(jnp.log1p(-jnp.exp(safe)) * valid * wrong[:, :, None]) / jnp.sum(
        counts * wrong
    )
    normed = -jnp.mean(jnp.sum(jax.nn.log_softmax(average, axis=-1) * correct, axis=-1))
    return likely + unlikely + normed


def pair_merge(first, second):
    first_max, first_sum, first_target = first
    second_max, second_sum, second_target = second
    joint_max = jnp.maximum(first_max, second_max)
    joint_sum = first_sum * jnp.exp(first_max - joint_max) + second_sum * jnp.exp(
        second_max - joint_max
    )
    return (joint_max, joint_sum, first_target + second_target)


def per_device(
    hidden_in,
    ff_gain,
    w_gate,
    w_up,
    w_out,
    ff_rescale,
    final_gain,
    w_head,
    targets,
    lengths,
    labels,
):
    place = lax.axis_index("mp")
    contract = (((1,), (1,)), ((), ()))
    inputs = hidden_in.astype(jnp.float32)
    normed_in = rms_scale(inputs, ff_gain)[0].astype(jnp.bfloat16)
    width = w_gate.shape[1]
    shard_rows = gathered_copies(normed_in, "mp", 0)
    gate_part = jnp.dot(shard_rows, w_gate, preferred_element_type=jnp.float32)
    up_part = jnp.dot(shard_rows, w_up, preferred_element_type=jnp.float32)
    projected = jnp.concatenate([gate_part, up_part], axis=1)
    activated = jax.nn.gelu(projected[:, :width], approximate=True) * projected[:, width:]
    hidden = (activated * ff_rescale).astype(jnp.bfloat16)
    residual = (
        summed_on_arrival(jnp.dot(hidden, w_out, preferred_element_type=jnp.float32), "mp", 0)
        + inputs
    )
    normed_out, inverse = rms_scale(residual, final_gain)
    logits = jnp.dot(
        gathered_copies(normed_out.astype(jnp.bfloat16), "mp", 0),
        w_head,
        preferred_element_type=jnp.float32,
    )
    vocab_own = logits.shape[1]
    columns = jnp.arange(vocab_own, dtype=jnp.int32)[None, :]
    is_target = columns == (targets - place * vocab_own)[:, None]
    target_part = jnp.sum(jnp.where(is_target, logits, 0.0), axis=1)
    local_max = jnp.max(logits, axis=1)
    local_sum = jnp.sum(jnp.exp(logits - local_max[:, None]), axis=1)
    row_max, row_sum, target_logit = combined_all(
        (local_max, local_sum, target_part), "mp", pair_merge
    )
    log_norm = row_max + jnp.log(row_sum)
    log_probs = target_logit - log_norm
    loss_value, pullback = jax.vjp(lambda values: task_loss(values, lengths, labels), log_probs)
    (token_weight,) = pullback(jnp.ones_like(loss_value))
    softmax_rows = jnp.exp(logits - log_norm[:, None])
    logit_grad = (token_weight[:, None] * (is_target.astype(jnp.float32) - softmax_rows)).astype(
        jnp.bfloat16
    )
    normed_grad = summed_on_arrival(
        lax.dot_general(logit_grad, w_head, contract, preferred_element_type=jnp.float32), "mp", 0
    )
    resid_grad = norm_back(residual, inverse, final_gain, normed_grad).astype(jnp.bfloat16)
    hidden_grad = lax.dot_general(
        lax.all_gather(resid_grad, "mp", axis=0, tiled=True),
        w_out,
        contract,
        preferred_element_type=jnp.float32,
    )
    scale_grad = jnp.sum(hidden_grad * activated, axis=0)
    return (scale_grad, loss_value.reshape(1))


def solution(mesh):
    return jax.shard_map(
        per_device,
        mesh=mesh,
        in_specs=(
            P(("task", "mp"), None),
            P(),
            P(None, "mp"),
            P(None, "mp"),
            P("mp", None),
            P(("task", "mp")),
            P(),
            P(None, "mp"),
            P("task"),
            P("task", None),
            P("task"),
        ),
        out_specs=(P(("task", "mp")), P("task")),
        check_vma=False,
    )
```

profile of v0, /device:TPU:1, one launch (start us, length us, event | category | flops | bytes accessed | tf_op | source)
XLA Modules:
  0.0 303.6 jit_solution(508517285441279573)
XLA Ops:
  7.2 1.2 fusion.14
  8.3 1.1 fusion.16
  9.4 0.3 broadcast_in_dim.32
  9.7 32.7 %all_to_all.20 = bf16[8,128,1024]{2,1,0:T(8,128)(2,1)S(1)} all-to-all(bf16[8,128,1024]{2,1,0:T(8,128)(2,1)S(1)} %broadcast_in_dim.32), channel_id=1, replica_groups=mesh['task'=32,'mp'=8] {'mp'}, dimensions={0} | all-to-all | bytes 4194304 | tf_op jit(solution)/shard_map/all_to_all | solution.py:11
  42.4 1.2 fusion.24
  43.7 1.4 fusion.11
  45.1 1.3 fusion.12
  46.4 50.9 %all_to_all.21 = f32[8,128,1024]{2,1,0:T(8,128)} all-to-all(f32[8,128,1024]{2,1,0:T(8,128)S(1)} %bitcast.39), channel_id=1, replica_groups=mesh['task'=32,'mp'=8] {'mp'}, dimensions={0} | all-to-all | bytes 8388608 | tf_op jit(solution)/shard_map/all_to_all | solution.py:33
  97.3 2.6 reduce_sum.156
  100.0 0.2 multiply_reduce_fusion.2
  100.2 0.1 multiply_convert_fusion.4
  100.3 1.6 broadcast_in_dim.56
  101.9 4.5 %all-to-all-start.2 = ((bf16[8,128,1024]{2,1,0:T(8,128)(2,1)}), bf16[8,128,1024]{2,1,0:T(8,128)(2,1)}, u32[]{:S(2)}, u32[]{:S(2)}) async-start(bf16[8,128,1024]{2,1,0:T(8,128)(2,1)} %broadcast_in_dim.56), calls=%async_computation.2 | async-start | bytes 4194304 | tf_op jit(solution)/shard_map/all_to_all | solution.py:11
  106.5 0.1 lt.41
  106.8 23.6 %all-to-all-done.2 = bf16[8,128,1024]{2,1,0:T(8,128)(2,1)} async-done(((bf16[8,128,1024]{2,1,0:T(8,128)(2,1)}), bf16[8,128,1024]{2,1,0:T(8,128)(2,1)}, u32[]{:S(2)}, u32[]{:S(2)}) %all-to-all-start.2) | async-done | bytes 2097184 | tf_op jit(solution)/shard_map/all_to_all | solution.py:11
  130.4 7.1 %fusion.23 = (f32[1024]{0:T(1024)S(1)}, f32[1024,2048]{1,0:T(8,128)S(1)}) fusion(bf16[1024,1024]{1,0:T(8,128)(2,1)} %bitcast.5, bf16[1024,2048]{1,0:T(8,128)(2,1)} %param.20), kind=kOutput, calls=%fused_computation.68 | convolution fusion | flops 4297063424 | bytes 14684160 | tf_op jit(solution)/shard_map/dot_general | solution.py:136
  137.5 2.6 exponential_reduce_fusion
  140.1 0.7 copy-done.2
  140.7 22.9 %all-gather.1 = f32[8,3,1024]{2,1,0:T(4,128)S(1)} all-gather(f32[1,3,1024]{2,1,0:T(4,128)S(1)} %maximum_bitcast_fusion), channel_id=2, replica_groups=mesh['task'=32,'mp'=8] {'mp'}, dimensions={0}, use_global_device_ids=true | all-gather | bytes 110592 | tf_op jit(solution)/shard_map/all_gather | solution.py:45
  163.8 0.6 while.19
  164.4 0.6 multiply_reduce_fusion.3
  165.1 0.2 select_reduce_fusion.1
  165.3 0.1 fusion.20
  165.4 0.2 exponential_reduce_fusion.1
  165.6 0.7 select_reduce_fusion.3
  168.0 8.8 %fusion = f32[1024,1024]{1,0:T(8,128)S(1)} fusion(bf16[1024,2048]{1,0:T(8,128)(2,1)} %param.20, f32[1024,2048]{1,0:T(8,128)} %copy-done.2, f32[1024]{0:T(1024)S(1)} %get-tuple-element.210, f32[1024]{0:T(1024)S(1)} %select_add_fusion, s32[1024]{0:T(1024)S(1)} %broadcast_subtract_fusion), kind=kOutput, calls=%fused_computation.8 | convolution fusion | flops 4307550208 | bytes 16789504 | tf_op jit(solution)/shard_map/dot_general | solution.py:159
  176.8 46.4 %all_to_all.22 = f32[8,128,1024]{2,1,0:T(8,128)} all-to-all(f32[8,128,1024]{2,1,0:T(8,128)S(1)} %bitcast.40), channel_id=1, replica_groups=mesh['task'=32,'mp'=8] {'mp'}, dimensions={0} | all-to-all | bytes 8388608 | tf_op jit(solution)/shard_map/all_to_all | solution.py:33
  223.2 3.4 %reduce_sum.165 = f32[128,1024]{1,0:T(8,128)} reduce(f32[8,128,1024]{2,1,0:T(8,128)} %all_to_all.22, f32[]{:T(128)} %constant.79.clone.1), dimensions={0}, to_apply=%region_14.15 | reduce | flops 917504 | bytes 4718596 | tf_op jit(solution)/shard_map/reduce_sum | solution.py:34
  226.6 1.2 multiply_reduce_fusion.1
  227.8 2.0 subtract_convert_fusion
  233.0 59.2 %all-gather.4.cloned.1.call-done = bf16[1024,1024]{1,0:T(8,128)(2,1)} async-done(((bf16[128,1024]{1,0:T(8,128)(2,1)}), bf16[1024,1024]{1,0:T(8,128)(2,1)}) %all-gather.4.cloned.1.call-update) | async-done | bytes 2097168 | tf_op jit(solution)/shard_map/all_gather | solution.py:163
  292.2 3.5 %multiply_reduce_fusion = f32[384]{0:T(512)} fusion(f32[1024,384]{1,0:T(8,128)S(1)} %fusion.11, bf16[1024,1024]{1,0:T(8,128)(2,1)} %all-gather.4.cloned.1.call-done, bf16[384,1024]{1,0:T(8,128)(2,1)S(1)} %copy-done), kind=kOutput, calls=%fused_computation.21 | convolution fusion | flops 806092416 | bytes 4457984 | tf_op jit(solution)/shard_map/dot_general | solution.py:162
  (71 shorter events, 1.3 us)
Async XLA Ops:
  7.2 38.0 %copy-start = (bf16[384,1024]{1,0:T(8,128)(2,1)S(1)}, bf16[384,1024]{1,0:T(8,128)(2,1)}, u32[]{:S(2)}) copy-start(bf16[384,1024]{1,0:T(8,128)(2,1)} %param.17) | copy-start | bytes 2359300
  9.7 32.7 %copy-start.8 = (bf16[1024,384]{1,0:T(8,128)(2,1)S(1)}, bf16[1024,384]{1,0:T(8,128)(2,1)}, u32[]{:S(2)}) copy-start(bf16[1024,384]{1,0:T(8,128)(2,1)} %param.15) | copy-start | bytes 2359300
  42.4 1.3 copy-start.9
  43.7 1.5 copy-start.5
  97.3 2.7 copy-start.1
  97.3 2.8 copy-start.4
  101.9 4.5 %copy-start.3 = (s32[4,4]{1,0:T(4,128)S(1)}, s32[4,4]{1,0:T(4,128)}, u32[]{:S(2)}) copy-start(s32[4,4]{1,0:T(4,128)} %param.22) | copy-start | bytes 196
  101.9 4.7 %copy-start.6 = (s32[4]{0:T(128)S(1)}, s32[4]{0:T(128)}, u32[]{:S(2)}) copy-start(s32[4]{0:T(128)} %param.23) | copy-start | bytes 52
  101.9 4.9 %copy-start.7 = (s32[1024]{0:T(1024)S(1)}, s32[1024]{0:T(1024)}, u32[]{:S(2)}) copy-start(s32[1024]{0:T(1024)} %param.21) | copy-start | bytes 12292
  101.9 28.6 %all-to-all-start.2 = ((bf16[8,128,1024]{2,1,0:T(8,128)(2,1)}), bf16[8,128,1024]{2,1,0:T(8,128)(2,1)}, u32[]{:S(2)}, u32[]{:S(2)}) async-start(bf16[8,128,1024]{2,1,0:T(8,128)(2,1)} %broadcast_in_dim.56), calls=%async_computation.2 | async-start | bytes 4194304 | tf_op jit(solution)/shard_map/all_to_all | solution.py:11
  106.3 185.8 %all-gather.4.cloned.1.call-start = ((), (), s32[]{:S(2)}) async-start(), calls=%async_computation.4 | async-start | bytes 2359296 | tf_op jit(solution)/shard_map/all_gather | solution.py:163
  137.5 3.2 %copy-start.2 = (f32[1024,2048]{1,0:T(8,128)}, f32[1024,2048]{1,0:T(8,128)S(1)}, u32[]{:S(2)}) copy-start(f32[1024,2048]{1,0:T(8,128)S(1)} %get-tuple-element.226) | copy-start | bytes 25165828
Sparse Core Ops, SparseCore 0:
  229.9 62.1 all-gather.3
where the time goes:
time: 304 us
  blocking collectives  153 us (50%)
  waiting for transfers between devices  82.9 us (27%)
  matrix products  23.3 us (8%)
  between operations  19.8 us (7%)
  other arithmetic  16.5 us (5%)
  starting transfers between devices  4.51 us (1%)
  local copies, waits for them, and re-layouts  3.4 us (1%)
    all_to_all x2, blocking collectives, summed_on_arrival(): pieces = lax.all_to_all(cut_along(x, dim, count), axis, 0, 0, tiled=True)  97.3 us
    all_gather x1, waiting for transfers between devices, per_device(): lax.all_gather(resid_grad, 'mp', axis=0, tiled=True)  59.2 us
    all_to_all x1, blocking collectives, sent_to_all(): return lax.all_to_all(copies, axis, split_axis=0, concat_axis=0, tiled=True)  32.7 us
    all_to_all x1, waiting for transfers between devices, sent_to_all(): return lax.all_to_all(copies, axis, split_axis=0, concat_axis=0, tiled=True)  23.6 us
    all_gather x1, blocking collectives, gathered_once(): both, at, found = (lax.all_gather(jnp.concatenate(lines), axis), 0, {})  22.9 us
    dot_general x1, matrix products, per_device(): lax.dot_general(logit_grad, w_head, contract, preferred_element_type=jnp....  8.8 us
    dot_general x1, matrix products, per_device(): jnp.dot(gathered_copies(normed_out.astype(jnp.bfloat16), 'mp', 0), w_head...  7.06 us
  transfers between devices with their start and end apart: 2, of which 2 were waited for; matrix products, arithmetic and copies ran while one was open for 0% of the time, Pallas kernels for 0%

commit v1 on v0

--- a/solution.py
+++ b/solution.py
@@ -160,7 +160,9 @@
     )
     resid_grad = norm_back(residual, inverse, final_gain, normed_grad).astype(jnp.bfloat16)
     hidden_grad = lax.dot_general(
-        lax.all_gather(resid_grad, "mp", axis=0, tiled=True),
+        jnp.concatenate(
+            lax.all_to_all(jnp.stack([resid_grad] * lax.axis_size("mp")), "mp", 0, 0), axis=0
+        ),
         w_out,
         contract,
         preferred_element_type=jnp.float32,

time: 304 us -> 260 us (0.86)
  the two profiles are of different devices: /device:TPU:1 before, /device:TPU:6 now
where the time goes in v1:
time: 260 us
  blocking collectives  159 us (61%)
  waiting for transfers between devices  41 us (16%)
  matrix products  23.3 us (9%)
  other arithmetic  15.8 us (6%)
  starting transfers between devices  8.81 us (3%)
  between operations  6.42 us (2%)
  local copies, waits for them, and re-layouts  4.96 us (2%)
    all_to_all x2, blocking collectives, summed_on_arrival(): pieces = lax.all_to_all(cut_along(x, dim, count), axis, 0, 0, tiled=True)  97.8 us
    all_to_all x1, blocking collectives, sent_to_all(): return lax.all_to_all(copies, axis, split_axis=0, concat_axis=0, tiled=True)  33 us
    all_gather x1, blocking collectives, gathered_once(): both, at, found = (lax.all_gather(jnp.concatenate(lines), axis), 0, {})  28.4 us
    all_to_all x1, waiting for transfers between devices, sent_to_all(): return lax.all_to_all(copies, axis, split_axis=0, concat_axis=0, tiled=True)  24.8 us
    all_to_all x1, waiting for transfers between devices, per_device(): lax.all_to_all(jnp.stack([resid_grad] * lax.axis_size('mp')), 'mp', 0, 0)  16.2 us
    dot_general x1, matrix products, per_device(): lax.dot_general(logit_grad, w_head, contract, preferred_element_type=jnp....  8.8 us
    dot_general x1, matrix products, per_device(): jnp.dot(gathered_copies(normed_out.astype(jnp.bfloat16), 'mp', 0), w_head...  7.06 us
    reduce_sum x2, other arithmetic, summed_on_arrival(): return jnp.sum(pieces, axis=0)  6.05 us
  transfers between devices with their start and end apart: 2, of which 2 were waited for; matrix products, arithmetic and copies ran while one was open for 0% of the time, Pallas kernels for 0%

profile of v1, /device:TPU:6, one launch (start us, length us, event | category | flops | bytes accessed | tf_op | source)
XLA Modules:
  0.0 259.7 jit_solution(9048340244180259038)
XLA Ops:
  0.6 1.2 fusion.14
  1.8 1.1 fusion.16
  2.9 0.3 broadcast_in_dim.32
  3.2 33.0 %all_to_all.25 = bf16[8,128,1024]{2,1,0:T(8,128)(2,1)S(1)} all-to-all(bf16[8,128,1024]{2,1,0:T(8,128)(2,1)S(1)} %broadcast_in_dim.32), channel_id=1, replica_groups=mesh['task'=32,'mp'=8] {'mp'}, dimensions={0} | all-to-all | bytes 4194304 | tf_op jit(solution)/shard_map/all_to_all | solution.py:11
  36.2 1.2 fusion.24
  37.5 1.4 fusion.11
  38.9 1.2 fusion.12
  40.2 51.8 %all_to_all.26 = f32[8,128,1024]{2,1,0:T(8,128)} all-to-all(f32[8,128,1024]{2,1,0:T(8,128)S(1)} %bitcast.40), channel_id=1, replica_groups=mesh['task'=32,'mp'=8] {'mp'}, dimensions={0} | all-to-all | bytes 8388608 | tf_op jit(solution)/shard_map/all_to_all | solution.py:33
  92.0 2.6 %reduce_sum.156 = f32[128,1024]{1,0:T(8,128)S(1)} reduce(f32[8,128,1024]{2,1,0:T(8,128)} %all_to_all.26, f32[]{:T(128)} %constant.79.clone.1), dimensions={0}, to_apply=%region_1.0 | reduce | flops 917504 | bytes 4718596 | tf_op jit(solution)/shard_map/reduce_sum | solution.py:34
  94.6 0.2 multiply_reduce_fusion.2
  94.9 1.6 broadcast_in_dim.56
  96.5 4.5 %all-to-all-start.2 = ((bf16[8,128,1024]{2,1,0:T(8,128)(2,1)}), bf16[8,128,1024]{2,1,0:T(8,128)(2,1)}, u32[]{:S(2)}, u32[]{:S(2)}) async-start(bf16[8,128,1024]{2,1,0:T(8,128)(2,1)} %broadcast_in_dim.56), calls=%async_computation.2 | async-start | bytes 4194304 | tf_op jit(solution)/shard_map/all_to_all | solution.py:11
  101.4 24.8 %all-to-all-done.2 = bf16[8,128,1024]{2,1,0:T(8,128)(2,1)} async-done(((bf16[8,128,1024]{2,1,0:T(8,128)(2,1)}), bf16[8,128,1024]{2,1,0:T(8,128)(2,1)}, u32[]{:S(2)}, u32[]{:S(2)}) %all-to-all-start.2) | async-done | bytes 2097184 | tf_op jit(solution)/shard_map/all_to_all | solution.py:11
  126.2 7.1 %fusion.23 = (f32[1024]{0:T(1024)S(1)}, f32[1024,2048]{1,0:T(8,128)S(1)}) fusion(bf16[1024,1024]{1,0:T(8,128)(2,1)} %bitcast.5, bf16[1024,2048]{1,0:T(8,128)(2,1)} %param.20), kind=kOutput, calls=%fused_computation.68 | convolution fusion | flops 4297063424 | bytes 14684160 | tf_op jit(solution)/shard_map/dot_general | solution.py:136
  133.3 2.6 exponential_reduce_fusion
  135.9 0.7 copy-done.2
  136.5 28.4 %all-gather.1 = f32[8,3,1024]{2,1,0:T(4,128)S(1)} all-gather(f32[1,3,1024]{2,1,0:T(4,128)S(1)} %maximum_bitcast_fusion), channel_id=2, replica_groups=mesh['task'=32,'mp'=8] {'mp'}, dimensions={0}, use_global_device_ids=true | all-gather | bytes 110592 | tf_op jit(solution)/shard_map/all_gather | solution.py:45
  165.1 0.6 while.19
  165.7 0.6 multiply_reduce_fusion.3
  166.4 0.2 select_reduce_fusion.1
  166.6 0.1 fusion.20
  166.7 0.2 exponential_reduce_fusion.1
  166.9 0.7 select_reduce_fusion.3
  169.3 8.8 %fusion = f32[1024,1024]{1,0:T(8,128)S(1)} fusion(bf16[1024,2048]{1,0:T(8,128)(2,1)} %param.20, f32[1024,2048]{1,0:T(8,128)} %copy-done.2, f32[1024]{0:T(1024)S(1)} %get-tuple-element.210, f32[1024]{0:T(1024)S(1)} %select_add_fusion, s32[1024]{0:T(1024)S(1)} %broadcast_subtract_fusion), kind=kOutput, calls=%fused_computation.8 | convolution fusion | flops 4307550208 | bytes 16789504 | tf_op jit(solution)/shard_map/dot_general | solution.py:159
  178.1 45.9 %all_to_all.27 = f32[8,128,1024]{2,1,0:T(8,128)} all-to-all(f32[8,128,1024]{2,1,0:T(8,128)S(1)} %bitcast.41), channel_id=1, replica_groups=mesh['task'=32,'mp'=8] {'mp'}, dimensions={0} | all-to-all | bytes 8388608 | tf_op jit(solution)/shard_map/all_to_all | solution.py:33
  224.1 3.4 %reduce_sum.165 = f32[128,1024]{1,0:T(8,128)} reduce(f32[8,128,1024]{2,1,0:T(8,128)} %all_to_all.27, f32[]{:T(128)} %constant.79.clone.1), dimensions={0}, to_apply=%region_14.15 | reduce | flops 917504 | bytes 4718596 | tf_op jit(solution)/shard_map/reduce_sum | solution.py:34
  227.5 1.2 multiply_reduce_fusion.1
  228.7 1.2 subtract_convert_fusion
  229.9 1.6 stack.2
  231.5 4.3 %all-to-all-start.4 = ((bf16[8,128,1024]{2,1,0:T(8,128)(2,1)}), bf16[8,128,1024]{2,1,0:T(8,128)(2,1)}, u32[]{:S(2)}, u32[]{:S(2)}) async-start(bf16[8,128,1024]{2,1,0:T(8,128)(2,1)} %stack.2), calls=%async_computation.4 | async-start | bytes 4194304 | tf_op jit(solution)/shard_map/all_to_all | solution.py:164
  239.0 16.2 %all-to-all-done.4 = bf16[8,128,1024]{2,1,0:T(8,128)(2,1)} async-done(((bf16[8,128,1024]{2,1,0:T(8,128)(2,1)}), bf16[8,128,1024]{2,1,0:T(8,128)(2,1)}, u32[]{:S(2)}, u32[]{:S(2)}) %all-to-all-start.4) | async-done | bytes 2097184 | tf_op jit(solution)/shard_map/all_to_all | solution.py:164
  255.1 3.5 %multiply_reduce_fusion = f32[384]{0:T(512)} fusion(f32[1024,384]{1,0:T(8,128)S(1)} %fusion.11, bf16[1024,1024]{1,0:T(8,128)(2,1)} %bitcast.14, bf16[384,1024]{1,0:T(8,128)(2,1)S(1)} %copy-done), kind=kOutput, calls=%fused_computation.21 | convolution fusion | flops 806092416 | bytes 4457984 | tf_op jit(solution)/shard_map/dot_general | solution.py:162
  (71 shorter events, 1.5 us)
Async XLA Ops:
  0.6 38.3 %copy-start = (bf16[384,1024]{1,0:T(8,128)(2,1)S(1)}, bf16[384,1024]{1,0:T(8,128)(2,1)}, u32[]{:S(2)}) copy-start(bf16[384,1024]{1,0:T(8,128)(2,1)} %param.17) | copy-start | bytes 2359300
  3.2 33.0 %copy-start.8 = (bf16[1024,384]{1,0:T(8,128)(2,1)S(1)}, bf16[1024,384]{1,0:T(8,128)(2,1)}, u32[]{:S(2)}) copy-start(bf16[1024,384]{1,0:T(8,128)(2,1)} %param.15) | copy-start | bytes 2359300
  36.2 1.3 copy-start.9
  37.4 1.5 copy-start.5
  92.0 2.7 %copy-start.1 = (bf16[128,1024]{1,0:T(8,128)(2,1)S(1)}, bf16[128,1024]{1,0:T(8,128)(2,1)}, u32[]{:S(2)}) copy-start(bf16[128,1024]{1,0:T(8,128)(2,1)} %param.13) | copy-start | bytes 786436
  92.0 2.8 %copy-start.4 = (f32[1024]{0:T(1024)S(1)}, f32[1024]{0:T(1024)}, u32[]{:S(2)}) copy-start(f32[1024]{0:T(1024)} %param.19) | copy-start | bytes 12292
  96.5 4.5 %copy-start.3 = (s32[4,4]{1,0:T(4,128)S(1)}, s32[4,4]{1,0:T(4,128)}, u32[]{:S(2)}) copy-start(s32[4,4]{1,0:T(4,128)} %param.22) | copy-start | bytes 196
  96.5 4.7 %copy-start.6 = (s32[4]{0:T(128)S(1)}, s32[4]{0:T(128)}, u32[]{:S(2)}) copy-start(s32[4]{0:T(128)} %param.23) | copy-start | bytes 52
  96.5 4.9 %copy-start.7 = (s32[1024]{0:T(1024)S(1)}, s32[1024]{0:T(1024)}, u32[]{:S(2)}) copy-start(s32[1024]{0:T(1024)} %param.21) | copy-start | bytes 12292
  96.5 29.7 %all-to-all-start.2 = ((bf16[8,128,1024]{2,1,0:T(8,128)(2,1)}), bf16[8,128,1024]{2,1,0:T(8,128)(2,1)}, u32[]{:S(2)}, u32[]{:S(2)}) async-start(bf16[8,128,1024]{2,1,0:T(8,128)(2,1)} %broadcast_in_dim.56), calls=%async_computation.2 | async-start | bytes 4194304 | tf_op jit(solution)/shard_map/all_to_all | solution.py:11
  133.3 3.2 %copy-start.2 = (f32[1024,2048]{1,0:T(8,128)}, f32[1024,2048]{1,0:T(8,128)S(1)}, u32[]{:S(2)}) copy-start(f32[1024,2048]{1,0:T(8,128)S(1)} %get-tuple-element.226) | copy-start | bytes 25165828
  231.5 23.7 %all-to-all-start.4 = ((bf16[8,128,1024]{2,1,0:T(8,128)(2,1)}), bf16[8,128,1024]{2,1,0:T(8,128)(2,1)}, u32[]{:S(2)}, u32[]{:S(2)}) async-start(bf16[8,128,1024]{2,1,0:T(8,128)(2,1)} %stack.2), calls=%async_computation.4 | async-start | bytes 4194304 | tf_op jit(solution)/shard_map/all_to_all | solution.py:164
